TPU v7x, 32 devices: a whole 2x2x4 slice. The times are simulated.
32 devices in a mesh: section: 4 (over z), ctx: 8 (over y, x, core).
Axes of the slice: x: 2, y: 2, z: 4, core: 2. Of those that a mesh axis runs over, the one named last changes fastest.
Arguments:
- queries: bfloat16 [4, 1024, 4096], P('section', 'ctx'), may hold values from -130 to 130
- keys_new: bfloat16 [4, 1024, 1024], P('section', 'ctx'), may hold values from -6 to 6
- values_new: bfloat16 [4, 1024, 1024], P('section', 'ctx'), may hold values from -6 to 6
- stretch_cache: bfloat16 [4, 512, 2048], P('section'), may hold values from -6 to 6
- hadamard_signs: int32 [4, 2, 128], P('section'), may hold values from -1 to 1, as said below
- stretch_docs: int32 [8], replicated, may hold values from 0 to 1, never falling along the last dimension, each value on 1 to 5 neighbouring positions
Outputs:
- handed: bfloat16 [4, 1024, 4096], P('section', 'ctx')
Inputs may be any that keep to these rules, and one draw needn't show every extreme that they name: `hadamard_signs`: each entry is -1 or 1. `stretch_docs`: never falling along the stretches; each document covers 1 to 5 stretches in a row.
All inputs are finite; a program needn't handle non-finite values.
Results may differ from a plain program's by a relative error of at most 0.0099.
Values may be sent and summed in bfloat16 or wider, within the bound.
A program may use at most 128 MiB of HBM per device.

v0:
```python
import math

import jax
import jax.numpy as jnp
import numpy as np
from jax import lax
from jax.sharding import PartitionSpec as P

CACHE = 256


def from_behind(block, axis, distance):
    devices = range(lax.axis_size(axis))
    route = [((i - distance) % len(devices), i) for i in devices]
    return lax.ppermute(block, axis, route)


def hadamard(length):
    numbers = np.arange(length)
    common = numbers[:, None] & numbers[None, :]
    parity = np.zeros((length, length), np.int64)
    for bit_place in range(max(int(length).bit_length(), 1)):
        parity = parity ^ common >> bit_place & 1
    return 1.0 - 2.0 * parity


def rotate(source, sign_row, rotation):
    row_count = source.shape[0]
    head_size = rotation.shape[0]
    shaped = (source.reshape(row_count, -1, head_size) * sign_row.astype(source.dtype)).reshape(
        -1, head_size
    )
    turned = jnp.dot(shaped, rotation, preferred_element_type=jnp.float32) * head_size ** (-0.5)
    return turned.reshape(row_count, -1).astype(jnp.bfloat16)


def attend(running, query_turned, key_rows, visible):
    row_max, row_sum, weighted = running
    kv_heads = query_turned.shape[1]
    head_size = query_turned.shape[3]
    key_part = key_rows[:, : kv_heads * head_size].reshape(-1, kv_heads, head_size)
    value_part = key_rows[:, kv_heads * head_size :].reshape(-1, kv_heads, head_size)
    scores = jnp.einsum(
        "rkgd,nkd->rkgn", query_turned, key_part, preferred_element_type=jnp.float32
    ) * head_size ** (-0.5)
    scores = jnp.where(visible[:, None, None, :], scores, -jnp.inf)
    new_max = jnp.maximum(row_max, scores.max(-1))
    factor = jnp.exp(row_max - new_max)
    exponent = jnp.exp(scores - new_max[..., None])
    row_sum = row_sum * factor + exponent.sum(-1)
    weighted = weighted * factor[..., None] + jnp.einsum(
        "rkgn,nkd->rkgd",
        exponent.astype(jnp.bfloat16),
        value_part,
        preferred_element_type=jnp.float32,
    )
    return (new_max, row_sum, weighted)


def attend_columns(running, query_turned, key_rows, allowed):
    visible = jnp.broadcast_to(allowed[None, :], (query_turned.shape[0], key_rows.shape[0]))
    return lax.cond(
        jnp.any(allowed),
        lambda state: attend(state, query_turned, key_rows, visible),
        lambda state: state,
        running,
    )


def doc_lookup(stretch_docs, stretch_ids, sources):
    return jnp.sum(
        jnp.where(sources[:, None] == stretch_ids[None, :], stretch_docs[None, :], 0), axis=1
    )


def per_device(queries, keys_new, values_new, stretch_cache, hadamard_signs, stretch_docs):
    head_size = hadamard_signs.shape[-1]
    rotation = jnp.asarray(hadamard(head_size), dtype=jnp.bfloat16)
    inverse = jnp.asarray(hadamard(head_size), dtype=jnp.float32)
    sign_keys = hadamard_signs[0, 0]
    sign_values = hadamard_signs[0, 1]
    query_rows = queries[0]
    row_total = query_rows.shape[0]
    kv_width = keys_new.shape[-1]
    kv_heads = kv_width // head_size
    groups = query_rows.shape[-1] // kv_width
    new_front = jnp.concatenate(
        [rotate(keys_new[0], sign_keys, rotation), rotate(values_new[0], sign_values, rotation)],
        axis=1,
    )
    query_turned = rotate(query_rows, sign_keys, rotation).reshape(
        row_total, kv_heads, groups, head_size
    )
    my_stretch = lax.axis_index("ctx")
    stretch_ids = jnp.arange(stretch_docs.shape[0], dtype=jnp.int32)
    my_doc = jnp.sum(jnp.where(stretch_ids == my_stretch, stretch_docs, 0))
    query_row = jnp.arange(row_total, dtype=jnp.int32)
    running = (
        jnp.full((row_total, kv_heads, groups), -jnp.inf, jnp.float32),
        jnp.zeros((row_total, kv_heads, groups), jnp.float32),
        jnp.zeros((row_total, kv_heads, groups, head_size), jnp.float32),
    )
    own_visible = query_row[None, :] <= query_row[:, None]
    running = attend(running, query_turned, new_front, own_visible)
    cache_rows = lax.dynamic_slice_in_dim(stretch_cache[0], my_doc * CACHE, CACHE, 0)
    cache_step_rows = math.gcd(cache_rows.shape[0], 512)
    cache_blocks = cache_rows.reshape(-1, cache_step_rows, cache_rows.shape[-1])
    full_visible = jnp.ones((row_total, cache_step_rows), dtype=bool)

    def cache_step(state, key_rows):
        return (attend(state, query_turned, key_rows, full_visible), None)

    running, _ = lax.scan(cache_step, running, cache_blocks)
    state = running
    portion = lax.all_gather(new_front, "ctx", axis=0, tiled=True)
    portion_rows = portion.shape[0]
    block_rows = math.gcd(portion_rows, 512)
    offsets = block_rows * jnp.arange(portion_rows // block_rows, dtype=jnp.int32)

    def inner_step(inner_state, item):
        key_rows, offset = item
        sources = (offset + jnp.arange(block_rows, dtype=jnp.int32)) // row_total
        allowed = (sources < my_stretch) & (
            doc_lookup(stretch_docs, stretch_ids, sources) == my_doc
        )
        return (attend_columns(inner_state, query_turned, key_rows, allowed), None)

    state, _ = lax.scan(
        inner_step, state, (portion.reshape(-1, block_rows, portion.shape[-1]), offsets)
    )
    running = state
    row_max, row_sum, weighted = running
    averaged = weighted / row_sum[..., None]
    restored = jnp.dot(averaged.reshape(-1, head_size), inverse, precision=lax.Precision.HIGHEST)
    restored = restored * head_size ** (-0.5) * sign_values.astype(jnp.float32)
    heads_out = restored.reshape(row_total, -1).astype(jnp.bfloat16)
    handed = from_behind(heads_out, "section", 1)
    return handed[None]


def solution(mesh):
    in_specs = (
        P("section", "ctx", None),
        P("section", "ctx", None),
        P("section", "ctx", None),
        P("section", None, None),
        P("section", None, None),
        P(),
    )
    out_specs = P("section", "ctx", None)
    return jax.shard_map(
        per_device, mesh=mesh, in_specs=in_specs, out_specs=out_specs, check_vma=False
    )
```

profile of v0, /device:TPU:2, one launch (start us, length us, event | category | flops | bytes accessed | tf_op | source)
XLA Modules:
  0.0 117.7 jit_solution(2856623178247255704)
XLA Ops:
  8.1 1.1 reshape_squeeze.9
  9.1 1.1 reshape_squeeze.11
  14.7 1.0 copy.54
  15.7 1.6 %reshape_squeeze.10 = bf16[4096,128]{1,0:T(8,128)(2,1)S(1)} reshape(bf16[1,128,4096]{2,1,0:T(8,128)(2,1)} %param.12) | data formatting | bytes 2097152 | tf_op jit(solution)/shard_map/reshape;squeeze | solution.py:30
  17.3 2.0 %copy.59 = bf16[256,1024]{0,1:T(8,128)(2,1)} copy(bf16[256,1024]{1,0:T(8,128)(2,1)} %get-tuple-element.452) | data formatting | bytes 1048576 | tf_op jit(solution)/shard_map/while/body/eval_jaxpr/slice | solution.py:42
  24.5 2.0 %bitcast_add_fusion.1 = f32[128,8,4,128]{0,3,2,1:T(8,128)} fusion(f32[8,128,128,4]{2,1,3,0:T(8,128)S(1)} %fusion.23, f32[128,8,4,128]{0,3,2,1:T(8,128)S(1)} %get-tuple-element.456, f32[128,8,4]{0,2,1:T(4,128)S(1)} %get-tuple-element.447, f32[128,8,4]{0,2,1:T(4,128)S(1)} %get-tuple-element.454, f32[128,8,4]{0,2,1:T(4,128)S(1)} %get-tuple-element.455, ...), kind=kOutput, calls=%fused_computation.46 | convolution fusion | flops 136839168 | bytes 6602752 | tf_op jit(solution)/shard_map/rkgn,nkd->rkgd/dot_general | solution.py:51
  26.5 3.0 %copy.61 = f32[128,8,4,128]{3,0,2,1:T(8,128)} copy(f32[128,8,4,128]{0,3,2,1:T(8,128)} %bitcast_add_fusion.1) | data formatting | bytes 4194304
  29.5 21.0 %all-gather.2.cloned.1.call-done = bf16[1024,2048]{1,0:T(8,128)(2,1)} async-done(((bf16[128,2048]{1,0:T(8,128)(2,1)}), bf16[1024,2048]{1,0:T(8,128)(2,1)}) %all-gather.2.cloned.1.call-update) | async-done | bytes 4194320 | tf_op jit(solution)/shard_map/all_gather | solution.py:115
  50.5 6.2 %copy.62 = bf16[2,512,2048]{1,2,0:T(8,128)(2,1)} copy(bf16[2,512,2048]{2,1,0:T(8,128)(2,1)} %bitcast.100) | data formatting | bytes 8388608
  56.7 19.5 %while.5 = (s32[]{:T(128)}, f32[128,8,4]{0,2,1:T(4,128)S(1)}, f32[128,8,4]{0,2,1:T(4,128)S(1)}, f32[128,8,4,128]{3,0,2,1:T(8,128)}, s32[2]{0:T(128)S(1)}, /*inde...) while((s32[]{:T(128)}, f32[128,8,4]{0,2,1:T(4,128)S(1)}, ...), condition=%wide.region_12.13_spmd.clone, body=%wide.region_5.12_spmd.clone.sunk | while | flops 1097907200 | bytes 57951640 | solution.py:128
  58.1 1.9 %and_reduce_fusion.3 = pred[]{:T(512)} fusion(s32[512]{0:T(512)S(1)} %select_reduce_fusion.2, s32[]{:T(128)} %get-tuple-element.565, s32[]{:T(128)} %get-tuple-element.563, s32[]{:T(128)} %bitcast.92), kind=kLoop, calls=%fused_computation.35.clone.1 | loop fusion | flops 10239 | bytes 2061 | tf_op jit(solution)/shard_map/while/body/eval_jaxpr/reduce_or | solution.py:63
  60.5 11.8 %conditional.3 = ((f32[128,8,4]{0,2,1:T(4,128)S(1)}, f32[128,8,4]{0,2,1:T(4,128)S(1)}, f32[128,8,4,128]{3,0,2,1:T(8,128)})) conditional(s32[]{:T(128)} %convert_element_type.97, (f32[128,8,4]{0,2,1:T(4,128)S(1)}, f32[128,8,4]{0,2,1:T(4,128)S(1)}, f32[128,8,4,128]{3,0,2,1:T(8,128)}) %tuple.62, (s32[]{:T(128)}, s32[1,512]{1,0:T(1,128)S(1)}, ...), branch_computations={%region_8.8_spmd, %region_9.11_spmd.clone} | conditional | flops 1097876992 | bytes 57941100 | solution.py:62
  61.8 1.7 %dynamic-slice_bitcast_fusion = bf16[512,2048]{0,1:T(8,128)(2,1)S(1)} fusion(bf16[2,512,2048]{1,2,0:T(8,128)(2,1)} %get-tuple-element.337, s32[]{:T(128)} %get-tuple-element.338), kind=kLoop, calls=%fused_computation.13 | loop fusion | bytes 4194308 | tf_op jit(solution)/shard_map/while/body/jit(dynamic_index_in_dim)/squeeze | solution.py:128
  63.7 2.0 %bitcast_reduce_fusion = (f32[128,8,4]{0,2,1:T(4,128)S(1)}, f32[8,512,128,4]{2,1,3,0:T(8,128)S(1)}) fusion(pred[512]{0:T(512)(128)(4,1)S(1)} %and_reduce_fusion, bf16[512,8,128,1]{0,2,3,1:T(8,128)(2,1)S(1)} %bitcast.93, bf16[128,8,4,128]{3,0,2,1:T(8,128)(2,1)S(1)} %get-tuple-element.339), kind=kOutput, calls=%fused_computation.2 | convolution fusion | flops 543158272 | bytes 10502656 | tf_op jit(solution)/shard_map/while/body/eval_jaxpr/cond/branch_1_fun/rkgd,nkd->rkgn/dot_general | solution.py:43
  65.7 2.0 %fusion.4 = f32[128,8,4]{0,2,1:T(4,128)S(1)} fusion(f32[8,512,128,4]{2,1,3,0:T(8,128)S(1)} %get-tuple-element.451, f32[128,8,4]{0,2,1:T(4,128)S(1)} %max.17, pred[512]{0:T(512)(128)(4,1)S(1)} %and_reduce_fusion), kind=kLoop, calls=%fused_computation.6 | loop fusion | flops 8384512 | bytes 8421888 | tf_op jit(solution)/shard_map/while/body/eval_jaxpr/cond/branch_1_fun/reduce_sum | solution.py:50
  67.8 3.1 %bitcast_add_fusion = f32[128,8,4,128]{3,0,2,1:T(8,128)S(1)} fusion(f32[128,8,4,128]{3,0,2,1:T(8,128)S(1)} %copy-done.1, bf16[512,8,128,1]{0,2,3,1:T(8,128)(2,1)S(1)} %bitcast.94, f32[8,512,128,4]{2,1,3,0:T(8,128)S(1)} %get-tuple-element.451, f32[128,8,4]{0,2,1:T(4,128)S(1)} %max.17, pred[512]{0:T(512)(128)(4,1)S(1)} %and_reduce_fusion, ...), kind=kOutput, calls=%fused_computation.12 | convolution fusion | flops 546308096 | bytes 13664768 | tf_op jit(solution)/shard_map/while/body/eval_jaxpr/cond/branch_1_fun/rkgn,nkd->rkgd/dot_general | solution.py:51
  71.0 1.4 %copy-done.2 = f32[128,8,4,128]{3,0,2,1:T(8,128)} copy-done((f32[128,8,4,128]{3,0,2,1:T(8,128)}, f32[128,8,4,128]{3,0,2,1:T(8,128)S(1)}, u32[]{:S(2)}) %copy-start.2) | copy-done | bytes 2097176 | tf_op jit(solution)/shard_map/while/body/eval_jaxpr/cond
  73.7 1.9 %and_reduce_fusion.3 = pred[]{:T(512)} fusion(s32[512]{0:T(512)S(1)} %select_reduce_fusion.2, s32[]{:T(128)} %get-tuple-element.565, s32[]{:T(128)} %get-tuple-element.563, s32[]{:T(128)} %bitcast.92), kind=kLoop, calls=%fused_computation.35.clone.1 | loop fusion | flops 10239 | bytes 2061 | tf_op jit(solution)/shard_map/while/body/eval_jaxpr/reduce_or | solution.py:63
  76.2 1.9 %broadcast_divide_fusion = f32[128,8,4,128]{3,0,2,1:T(8,128)S(1)} fusion(f32[128,8,4,128]{3,0,2,1:T(8,128)} %get-tuple-element.327, f32[128,8,4]{0,2,1:T(4,128)S(1)} %get-tuple-element.328), kind=kLoop, calls=%fused_computation.59 | loop fusion | flops 524288 | bytes 4210688 | tf_op jit(solution)/shard_map/div | solution.py:133
  78.2 1.4 %copy.64 = f32[128,8,4,128]{3,2,1,0:T(4,128)S(1)} copy(f32[128,8,4,128]{3,0,2,1:T(8,128)S(1)} %broadcast_divide_fusion) | data formatting | bytes 4194304 | tf_op jit(solution)/shard_map/div | solution.py:133
  79.5 1.8 %fusion.19 = bf16[4096,128]{1,0:T(8,128)(2,1)S(1)} fusion(f32[4096,128]{1,0:T(8,128)S(1)} %bitcast.98, f32[128,128]{1,0:T(8,128)S(1)} %copy-done.8, f32[128]{0:T(128)S(1)} %multiply_bitcast_fusion), kind=kOutput, calls=%fused_computation.39 | convolution fusion | flops 806354944 | bytes 3211776 | tf_op jit(solution)/shard_map/dot_general | solution.py:134
  81.3 1.3 %convert_element_type.79 = bf16[128,4096]{1,0:T(8,128)(2,1)} reshape(bf16[4096,128]{1,0:T(8,128)(2,1)S(1)} %fusion.19) | data formatting | bytes 2097152 | tf_op jit(solution)/shard_map/convert_element_type | solution.py:136
  82.6 1.5 %collective-permute-start = (bf16[128,4096]{1,0:T(8,128)(2,1)}, bf16[128,4096]{1,0:T(8,128)(2,1)S(1)}, u32[]{:S(2)}, u32[]{:S(2)}) collective-permute-start(bf16[128,4096]{1,0:T(8,128)(2,1)} %convert_element_type.79), channel_id=1, source_target_pairs={{24,0},{0,8},{8,16},{16,24},{25,1},{1,9},{9,17},{17,25},{26,2},{2,... | collective-permute-start | bytes 3145736 | tf_op jit(solution)/shard_map/ppermute | solution.py:15
  84.1 25.8 %collective-permute-done = bf16[128,4096]{1,0:T(8,128)(2,1)S(1)} collective-permute-done((bf16[128,4096]{1,0:T(8,128)(2,1)}, bf16[128,4096]{1,0:T(8,128)(2,1)S(1)}, u32[]{:S(2)}, u32[]{:S(2)}) %collective-permute-start) | collective-permute-done | bytes 1048608 | tf_op jit(solution)/shard_map/ppermute | solution.py:15
  (62 shorter events, 15.6 us)
Async XLA Ops:
  6.5 7.2 %copy-start = (bf16[1,512,2048]{2,1,0:T(8,128)(2,1)S(1)}, bf16[1,512,2048]{2,1,0:T(8,128)(2,1)}, u32[]{:S(2)}) copy-start(bf16[1,512,2048]{2,1,0:T(8,128)(2,1)} %param.15) | copy-start | bytes 6291460
  6.5 4.8 %copy-start.7 = (bf16[128,128]{1,0:T(8,128)(2,1)S(1)}, bf16[128,128]{1,0:T(8,128)(2,1)}, u32[]{:S(2)}) copy-start(bf16[128,128]{1,0:T(8,128)(2,1)} %constant.108.clone) | copy-start | bytes 98308
  6.5 44.0 %all-gather.2.cloned.1.call-start = ((), (), s32[]{:S(2)}) async-start(), calls=%async_computation | async-start | bytes 4718592 | tf_op jit(solution)/shard_map/all_gather | solution.py:115
  9.1 3.4 %copy-start.9 = (s32[8]{0:T(128)S(1)}, s32[8]{0:T(128)}, u32[]{:S(2)}) copy-start(s32[8]{0:T(128)} %param.17) | copy-start | bytes 100
  11.2 2.6 %copy-start.3 = (bf16[1024,128]{1,0:T(8,128)(2,1)}, bf16[1024,128]{1,0:T(8,128)(2,1)S(1)}, u32[]{:S(2)}) copy-start(bf16[1024,128]{1,0:T(8,128)(2,1)S(1)} %fusion.30) | copy-start | bytes 786436
  19.3 0.9 copy-start.4
  20.1 1.1 copy-start.6
  22.5 1.1 copy-start.5
  26.5 3.0 %copy-start.10 = (s32[1,2,128]{2,1,0:T(2,128)S(1)}, s32[1,2,128]{2,1,0:T(2,128)}, u32[]{:S(2)}) copy-start(s32[1,2,128]{2,1,0:T(2,128)} %param.16) | copy-start | bytes 3076
  65.7 2.1 %copy-start.1 = (f32[128,8,4,128]{3,0,2,1:T(8,128)S(1)}, f32[128,8,4,128]{3,0,2,1:T(8,128)}, u32[]{:S(2)}) copy-start(f32[128,8,4,128]{3,0,2,1:T(8,128)} %get-tuple-element.341) | copy-start | bytes 6291460 | tf_op jit(solution)/shard_map/while/body/eval_jaxpr/cond
  71.0 1.4 %copy-start.2 = (f32[128,8,4,128]{3,0,2,1:T(8,128)}, f32[128,8,4,128]{3,0,2,1:T(8,128)S(1)}, u32[]{:S(2)}) copy-start(f32[128,8,4,128]{3,0,2,1:T(8,128)S(1)} %bitcast_add_fusion) | copy-start | bytes 6291460 | tf_op jit(solution)/shard_map/while/body/eval_jaxpr/cond
  78.1 1.4 %copy-start.8 = (f32[128,128]{1,0:T(8,128)S(1)}, f32[128,128]{1,0:T(8,128)}, u32[]{:S(2)}) copy-start(f32[128,128]{1,0:T(8,128)} %constant.109.clone) | copy-start | bytes 196612
  82.6 27.3 %collective-permute-start = (bf16[128,4096]{1,0:T(8,128)(2,1)}, bf16[128,4096]{1,0:T(8,128)(2,1)S(1)}, u32[]{:S(2)}, u32[]{:S(2)}) collective-permute-start(bf16[128,4096]{1,0:T(8,128)(2,1)} %convert_element_type.79), channel_id=1, source_target_pairs={{24,0},{0,8},{8,16},{16,24},{25,1},{1,9},{9,17},{17,25},{26,2},{2,... | collective-permute-start | bytes 3145736 | tf_op jit(solution)/shard_map/ppermute | solution.py:15
Sparse Core Ops, SparseCore 0:
  12.7 37.7 all-gather.1
where the time goes:
time: 118 us
  waiting for transfers between devices  46.9 us (40%)
  local copies, waits for them, and re-layouts  26.2 us (22%)
  other arithmetic  14.7 us (12%)
  between operations  14.2 us (12%)
  matrix products  13 us (11%)
  starting transfers between devices  1.49 us (1%)
  loops' own time  1.35 us (1%)
    ppermute x1, waiting for transfers between devices, from_behind(): return lax.ppermute(block, axis, route)  25.8 us
    all_gather x1, waiting for transfers between devices, per_device(): portion = lax.all_gather(new_front, 'ctx', axis=0, tiled=True)  21 us
    unnamed x21, local copies, waits for them, and re-layouts  10.8 us
    dot_general x3, matrix products, attend(): jnp.einsum('rkgn,nkd->rkgd', exponent.astype(jnp.bfloat16), value_part, p...  6.08 us
    reduce_or x2, other arithmetic, attend_columns(): jnp.any(allowed)  3.73 us
    another operation x3, local copies, waits for them, and re-layouts, rotate(): source.reshape(row_count, -1, head_size) * sign_row.astype(source.dtype)  3.69 us
    dot_general x3, matrix products, attend(): jnp.einsum('rkgd,nkd->rkgn', query_turned, key_part, preferred_element_ty...  3.55 us
    reduce_sum x3, other arithmetic, attend(): row_sum = row_sum * factor + exponent.sum(-1)  3.25 us
  transfers between devices with their start and end apart: 2, of which 2 were waited for; matrix products, arithmetic and copies ran while one was open for 13% of the time, Pallas kernels for 0%

commit v1 on v0

v1 whole, which is shorter than its diff:
```python
import functools

import jax
import jax.numpy as jnp
import numpy as np
from jax import lax
from jax.experimental import pallas as pl
from jax.experimental.pallas import tpu as pltpu
from jax.sharding import PartitionSpec as P

CACHE = 256
MESH = pl.DeviceIdType.MESH


def hadamard(length):
    numbers = np.arange(length)
    common = numbers[:, None] & numbers[None, :]
    parity = np.zeros((length, length), np.int64)
    for bit_place in range(max(int(length).bit_length(), 1)):
        parity = parity ^ common >> bit_place & 1
    return 1.0 - 2.0 * parity


def attention_kernel(
    n,
    sections,
    docs_ref,
    signs_ref,
    hada_ref,
    q_hbm,
    k_hbm,
    v_hbm,
    cache_hbm,
    out_hbm,
    q_buf,
    cache_buf,
    own,
    held,
    out_buf,
    load_sem,
    own_sem,
    send_sem,
    recv_sem,
    out_send,
    out_recv,
):
    section = lax.axis_index("section")
    me = lax.axis_index("ctx")
    odd = lax.rem(me, 2)
    reach = held.shape[0]
    half = reach // 2
    heads = own.shape[0]
    rows, hd = own.shape[2], own.shape[3]
    width = out_buf.shape[2]
    groups = width // hd
    kv_width = heads * hd
    detour = n == 8

    def cols(start, size):
        return pl.ds(pl.multiple_of(start, hd), size)

    def own_copies(h):
        return (
            pltpu.make_async_copy(k_hbm.at[:, cols(h * hd, hd)], own.at[h, 0], own_sem.at[h, 0]),
            pltpu.make_async_copy(v_hbm.at[:, cols(h * hd, hd)], own.at[h, 1], own_sem.at[h, 1]),
        )

    def start_own(h, carry):
        for copy in own_copies(h):
            copy.start()
        return carry

    lax.fori_loop(0, heads, start_own, 0)
    cache_copy = pltpu.make_async_copy(cache_hbm, cache_buf, load_sem.at[0])
    cache_copy.start()
    q_copy = pltpu.make_async_copy(q_hbm, q_buf, load_sem.at[1])
    q_copy.start()

    barrier = pltpu.get_barrier_semaphore()
    sibling = me + 1 - 2 * odd
    following = lax.rem(section + 1, sections)
    previous = lax.rem(section + sections - 1, sections)

    def greet(sec, ctx):
        pl.semaphore_signal(barrier, inc=1, device_id=(sec, ctx), device_id_type=MESH)

    greet(section, sibling)
    greet(following, me)
    greet(previous, me)
    count = jnp.int32(3)
    for e in range(2, reach + 1, 2):
        @pl.when(me + e < n)
        def _(e=e):
            greet(section, me + e)

        @pl.when(me >= e)
        def _(e=e):
            greet(section, me - e)

        count = count + jnp.where(me + e < n, 1, 0) + jnp.where(me >= e, 1, 0)
    pl.semaphore_wait(barrier, count)

    def remote(src, row, h, target, distance):
        return pltpu.make_async_remote_copy(
            src_ref=src,
            dst_ref=held.at[distance - 1, h],
            send_sem=send_sem.at[row, h],
            recv_sem=recv_sem.at[distance - 1, h],
            device_id=(section, target),
            device_id_type=MESH,
        )

    def own_sends(h, act):
        for e in range(2, reach + 1, 2):
            go = me + e < n
            if detour and e == 2:
                go = go & (me // 2 != 1)

            @pl.when(go)
            def _(e=e):
                act(remote(own.at[h], e // 2 - 1, h, me + e, e))

        @pl.when(odd == 0)
        def _():
            act(remote(own.at[h], half, h, me + 1, 1))

    def relay_sends(h, act, wait):
        for e in range(reach, 1, -2):
            @pl.when(me >= e)
            def _(e=e):
                block = held.at[e - 1, h]
                if wait:
                    remote(block, 0, h, me, e).wait_recv()
                if detour and e == 4:
                    @pl.when(me >= n - 2)
                    def _():
                        act(remote(block, reach + 1, h, me - 2, 2))

                @pl.when(odd == 1)
                def _():
                    act(remote(block, half + e // 2, h, me - 1, e - 1))

                if e < reach:
                    @pl.when(odd == 0)
                    def _():
                        act(remote(block, half + e // 2, h, me + 1, e + 1))

    def send_own(h, carry):
        for copy in own_copies(h):
            copy.wait()
        own_sends(h, lambda copy: copy.start())
        return carry

    lax.fori_loop(0, heads, send_own, 0)

    for d in range(1, reach + 1):
        @pl.when(me < d)
        def _(d=d):
            held[d - 1] = jnp.zeros(held.shape[1:], held.dtype)

    my_doc = docs_ref[me]
    biases = []
    for d in range(1, reach + 1):
        seen = (me >= d) & (docs_ref[jnp.maximum(me - d, 0)] == my_doc)
        biases.append(jnp.where(seen, 0.0, -jnp.inf).astype(jnp.float32))
    picks = [
        jnp.full((1, hd), jnp.where(my_doc == doc, 1.0, 0.0), jnp.float32).astype(jnp.bfloat16)
        for doc in range(cache_buf.shape[0] // CACHE)
    ]

    def cache_block(start):
        terms = [
            cache_buf[doc * CACHE : (doc + 1) * CACHE, cols(start, hd)] * pick
            for doc, pick in enumerate(picks)
        ]
        return functools.reduce(jnp.add, terms)

    root = hd ** -0.5
    sign_k = signs_ref[0:1, :].astype(jnp.float32) * root
    sign_v = signs_ref[1:2, :].astype(jnp.float32) * root
    hada = hada_ref[...]
    factor = root * float(np.log2(np.e))
    cache_copy.wait()
    q_copy.wait()
    relay_sends(0, lambda copy: copy.start(), True)

    def out_copy(h):
        return pltpu.make_async_remote_copy(
            src_ref=out_buf.at[h],
            dst_ref=out_hbm.at[:, cols(h * width, width)],
            send_sem=out_send.at[h],
            recv_sem=out_recv.at[h],
            device_id=(following, me),
            device_id_type=MESH,
        )

    causal = lax.broadcasted_iota(jnp.int32, (rows, rows), 1) <= lax.broadcasted_iota(
        jnp.int32, (rows, rows), 0
    )

    def head_step(h, carry):
        back_k = jnp.dot(cache_block(h * hd), hada, preferred_element_type=jnp.float32)
        back_v = jnp.dot(cache_block(kv_width + h * hd), hada, preferred_element_type=jnp.float32)
        back_k = (back_k * sign_k).astype(jnp.bfloat16)
        back_v = (back_v * sign_v).astype(jnp.bfloat16)
        for d in range(1, reach + 1, 2):
            @pl.when(me >= d)
            def _(d=d):
                remote(held.at[d - 1, h], 0, h, me, d).wait_recv()
        keys = jnp.concatenate(
            [back_k, own[h, 0]] + [held[d, h, 0] for d in range(reach)], axis=0
        )
        values = jnp.concatenate(
            [back_v, own[h, 1]] + [held[d, h, 1] for d in range(reach)], axis=0
        )
        for g in range(groups):
            if g == groups // 2:
                @pl.when(h + 1 < heads)
                def _():
                    relay_sends(h + 1, lambda copy: copy.start(), True)
            query = q_buf[:, cols(h * width + g * hd, hd)]
            scores = lax.dot_general(
                query, keys, (((1,), (1,)), ((), ())), preferred_element_type=jnp.float32
            )
            parts = [scores[:, at : at + rows] for at in range(0, CACHE, rows)]
            parts.append(jnp.where(causal, scores[:, CACHE : CACHE + rows], -jnp.inf))
            for d in range(reach):
                at = CACHE + rows * (d + 1)
                parts.append(scores[:, at : at + rows] + biases[d])
            top = functools.reduce(jnp.maximum, parts)
            top = jnp.max(top, axis=1, keepdims=True)
            expo = [jnp.exp2((part - top) * factor) for part in parts]
            total = jnp.sum(functools.reduce(jnp.add, expo), axis=1, keepdims=True)
            weights = jnp.concatenate([part.astype(jnp.bfloat16) for part in expo], axis=1)
            summed = jnp.dot(weights, values, preferred_element_type=jnp.float32)
            out_buf[h, :, g * hd : (g + 1) * hd] = (summed / total).astype(out_buf.dtype)
        out_copy(h).start()
        return carry

    lax.fori_loop(0, heads, head_step, 0)

    def finish(h, carry):
        own_sends(h, lambda copy: copy.wait_send())
        relay_sends(h, lambda copy: copy.wait_send(), False)
        out_copy(h).wait()
        return carry

    lax.fori_loop(0, heads, finish, 0)


def per_device(n, sections, queries, keys_new, values_new, stretch_cache, signs, docs):
    rows, q_width = queries.shape[1:]
    kv_width = keys_new.shape[-1]
    hd = signs.shape[-1]
    heads = kv_width // hd
    width = q_width // heads
    reach = n // 2
    dtype = queries.dtype
    anywhere = pl.BlockSpec(memory_space=pl.ANY)
    vmem = pl.BlockSpec(memory_space=pltpu.VMEM)
    out = pl.pallas_call(
        functools.partial(attention_kernel, n, sections),
        out_shape=jax.ShapeDtypeStruct((rows, q_width), dtype),
        in_specs=[pl.BlockSpec(memory_space=pltpu.SMEM), vmem, vmem] + [anywhere] * 4,
        out_specs=anywhere,
        scratch_shapes=[
            pltpu.VMEM((rows, q_width), dtype),
            pltpu.VMEM(stretch_cache.shape[1:], dtype),
            pltpu.VMEM((heads, 2, rows, hd), dtype),
            pltpu.VMEM((reach, heads, 2, rows, hd), dtype),
            pltpu.VMEM((heads, rows, width), dtype),
            pltpu.SemaphoreType.DMA((2,)),
            pltpu.SemaphoreType.DMA((heads, 2)),
            pltpu.SemaphoreType.DMA((reach + 2, heads)),
            pltpu.SemaphoreType.DMA((reach, heads)),
            pltpu.SemaphoreType.DMA((heads,)),
            pltpu.SemaphoreType.DMA((heads,)),
        ],
        compiler_params=pltpu.CompilerParams(
            collective_id=0, has_side_effects=True, vmem_limit_bytes=60 * 1024 * 1024
        ),
    )(
        docs,
        signs[0],
        jnp.asarray(hadamard(hd), dtype),
        queries[0],
        keys_new[0],
        values_new[0],
        stretch_cache[0],
    )
    return out[None]


def solution(mesh):
    in_specs = (
        P("section", "ctx", None),
        P("section", "ctx", None),
        P("section", "ctx", None),
        P("section", None, None),
        P("section", None, None),
        P(),
    )
    out_specs = P("section", "ctx", None)
    body = functools.partial(per_device, mesh.shape["ctx"], mesh.shape["section"])
    return jax.shard_map(body, mesh=mesh, in_specs=in_specs, out_specs=out_specs, check_vma=False)
```

time: 118 us -> 43.2 us (0.37)
  the two profiles are of different devices: /device:TPU:2 before, /device:TPU:4 now
where the time goes in v1:
time: 43.2 us; the launch traced here: 43 us
  Pallas kernels  40.7 us (94%)
  local copies, waits for them, and re-layouts  2.29 us (5%)
    pallas_call x1, Pallas kernels, per_device(): pl.pallas_call(functools.partial(attention_kernel, n, sections), out_shap...  40.7 us
    unnamed x1, local copies, waits for them, and re-layouts  2.29 us

profile of v1, /device:TPU:4, one launch (start us, length us, event | category | flops | bytes accessed | tf_op | source)
XLA Modules:
  0.0 43.0 jit_solution(5691947771040914473)
XLA Ops:
  0.0 40.7 %shard_map.73 = bf16[128,4096]{1,0:T(8,128)(2,1)} custom-call(s32[8]{0:T(128)} %docs_ref.1, s32[2,128]{1,0:T(2,128)} %bitcast.11, bf16[128,128]{1,0:T(8,128)(2,1)} %constant.2.clone.hada_ref, bf16[128,4096]{1,0:T(8,128)(2,1)} %bitcast.8, bf16[128,1024]{1,0:T(8,128)(2,1)} %bitcast.9, bf16[128,1024]{1,0:T(8,128)(2,1)} %bitcast.10, bf16[512,2048]{1,0:T(8,128)(2,1)} %bitcast.7), custom_call_target="tpu_custom_call" | custom-call | tf_op jit(solution)/shard_map/pallas_call | solution.py:261
  40.7 2.3 %copy.9 = bf16[1,128,4096]{2,1,0:T(8,128)(2,1)} copy(bf16[1,128,4096]{2,1,0:T(8,128)(2,1)} %bitcast.6) | data formatting | bytes 2097152
